TPU v7x, 32 devices: a whole 2x2x4 slice. The times are simulated.
32 devices in a mesh: sp: 4 (over z), tp: 8 (over y, x, core).
Axes of the slice: x: 2, y: 2, z: 4, core: 2. Of those that a mesh axis runs over, the one named last changes fastest.
Arguments:
- tokens: bfloat16 [8192, 2048], P(('sp', 'tp')), may hold values from -3 to 3
- queries: bfloat16 [8192, 2048], P(('sp', 'tp')), may hold values from -140 to 140
- keys: bfloat16 [8192, 1024], P(('sp', 'tp')), may hold values from -6 to 6
- values: bfloat16 [8192, 1024], P(('sp', 'tp')), may hold values from -6 to 6
- out_weight: bfloat16 [2048, 2048], P('sp', 'tp'), may hold values from -0.25 to 0.25
- norm_gain: bfloat16 [2048], replicated, may hold values from 0.099609375 to 1.8984375
- gate_weight: bfloat16 [2048, 7168], P('sp', 'tp'), may hold values from -0.125 to 0.125
- up_weight: bfloat16 [2048, 7168], P('sp', 'tp'), may hold values from -0.125 to 0.125
- down_weight: bfloat16 [7168, 2048], P('tp', 'sp'), may hold values from -0.125 to 0.125
Outputs:
- attended: bfloat16 [8192, 2048], P(('sp', 'tp'))
- layer_out: bfloat16 [8192, 2048], P(('sp', 'tp'))
All inputs are finite; a program needn't handle non-finite values.
Results may differ from a plain program's by a relative error of at most 0.023.
Values may be sent and summed in bfloat16 or wider, within the bound.
A program may use at most 256 MiB of HBM per device.

v0:
```python
import jax
import jax.numpy as jnp
from jax import lax
from jax.sharding import PartitionSpec as P

HEAD_DIM = 128
norm_eps = 1e-05


def attend(q_block, query_pos, k_block, v_block, key_pos, kv_local):
    row_count = q_block.shape[0]
    key_count = k_block.shape[0]
    q_four = q_block.reshape(row_count, kv_local, -1, HEAD_DIM)
    k_three = k_block.reshape(key_count, kv_local, HEAD_DIM)
    v_three = v_block.reshape(key_count, kv_local, HEAD_DIM)
    scores = jnp.einsum(
        "qhgd,khd->hgqk", q_four, k_three, preferred_element_type=jnp.float32
    ) * HEAD_DIM ** (-0.5)
    causal = key_pos[None, :] <= query_pos[:, None]
    scores = jnp.where(causal[None, None, :, :], scores, -1e30)
    row_peak = jnp.max(scores, axis=-1, keepdims=True)
    exp_terms = jnp.exp(scores - row_peak)
    probs = (exp_terms / jnp.sum(exp_terms, axis=-1, keepdims=True)).astype(jnp.bfloat16)
    mixed_out = jnp.einsum("hgqk,khd->qhgd", probs, v_three, preferred_element_type=jnp.float32)
    return mixed_out.astype(jnp.bfloat16).reshape(row_count, -1)


def add_rows(all_rows, weight_piece):
    return jnp.dot(all_rows, weight_piece, preferred_element_type=jnp.float32)


def shards(
    tokens, queries, keys, values, out_weight, norm_gain, gate_weight, up_weight, down_weight
):
    shard_rows = tokens.shape[0]
    sp_count = lax.axis_size("sp")
    tp_count = lax.axis_size("tp")
    segment_len = shard_rows * tp_count
    seq_len = segment_len * sp_count
    local_q = lax.all_to_all(queries, "sp", split_axis=1, concat_axis=0, tiled=True)
    part_keys, part_values = (
        lax.all_to_all(keys, "sp", split_axis=1, concat_axis=0, tiled=True),
        lax.all_to_all(values, "sp", split_axis=1, concat_axis=0, tiled=True),
    )
    width_kv = part_keys.shape[1]
    grid_keys, grid_values = (
        lax.all_gather(part_keys.reshape(sp_count, shard_rows, width_kv), "tp", axis=1, tiled=True),
        lax.all_gather(
            part_values.reshape(sp_count, shard_rows, width_kv), "tp", axis=1, tiled=True
        ),
    )
    all_keys = grid_keys.reshape(seq_len, width_kv)
    all_values = grid_values.reshape(seq_len, width_kv)
    kv_local = all_keys.shape[1] // HEAD_DIM
    query_index = jnp.arange(sp_count * shard_rows, dtype=jnp.int32)
    query_pos = (
        query_index // shard_rows * segment_len
        + lax.axis_index("tp") * shard_rows
        + query_index % shard_rows
    )
    key_pos = jnp.arange(seq_len, dtype=jnp.int32)
    pieces_out = []
    for segment in range(sp_count):
        first_row = segment * shard_rows
        key_reach = (segment + 1) * segment_len
        pieces_out.append(
            attend(
                local_q[first_row : first_row + shard_rows],
                query_pos[first_row : first_row + shard_rows],
                all_keys[:key_reach],
                all_values[:key_reach],
                key_pos[:key_reach],
                kv_local,
            )
        )
    attn = jnp.concatenate(pieces_out, axis=0)
    wo_full = lax.all_gather(out_weight, "tp", axis=1, tiled=True)
    block_rows = attn
    attn_part = lax.psum_scatter(
        jnp.dot(block_rows, wo_full, preferred_element_type=jnp.float32).astype(jnp.bfloat16),
        "sp",
        scatter_dimension=0,
        tiled=True,
    ).astype(jnp.float32)
    attended = (tokens.astype(jnp.float32) + attn_part).astype(jnp.bfloat16)
    attended_wide = attended.astype(jnp.float32)
    inverse_rms = lax.rsqrt(
        jnp.mean(attended_wide * attended_wide, axis=1, keepdims=True) + norm_eps
    )
    normed = (attended_wide * inverse_rms * norm_gain.astype(jnp.float32)).astype(jnp.bfloat16)
    all_rows = lax.all_gather(normed, "tp", axis=0, tiled=True)

    def add_single(weight_piece):
        return add_rows(all_rows, weight_piece)

    gate_sum = add_single(lax.all_gather(gate_weight, "sp", axis=0, tiled=True))
    up_sum = add_single(lax.all_gather(up_weight, "sp", axis=0, tiled=True))
    hidden = (jax.nn.silu(gate_sum) * up_sum).astype(jnp.bfloat16)
    down_full = lax.all_gather(down_weight, "sp", axis=1, tiled=True)
    block_rows = hidden
    ffn_part = lax.psum_scatter(
        jnp.dot(block_rows, down_full, preferred_element_type=jnp.float32).astype(jnp.bfloat16),
        "tp",
        scatter_dimension=0,
        tiled=True,
    ).astype(jnp.float32)
    layer_out = (attended_wide + ffn_part).astype(jnp.bfloat16)
    return (attended, layer_out)


def solution(mesh):
    return jax.shard_map(
        shards,
        mesh=mesh,
        in_specs=(
            P(("sp", "tp"), None),
            P(("sp", "tp"), None),
            P(("sp", "tp"), None),
            P(("sp", "tp"), None),
            P("sp", "tp"),
            P(),
            P("sp", "tp"),
            P("sp", "tp"),
            P("tp", "sp"),
        ),
        out_specs=(P(("sp", "tp"), None), P(("sp", "tp"), None)),
        check_vma=False,
    )
```

profile of v0, /device:TPU:0, one launch (start us, length us, event | category | flops | bytes accessed | tf_op | source)
XLA Modules:
  0.0 878.5 jit_solution(10126609819446409011)
XLA Ops:
  8.5 20.7 %all_to_all.48 = bf16[256,4,256]{0,2,1:T(8,128)(2,1)} all-to-all(bf16[256,4,256]{0,2,1:T(8,128)(2,1)S(1)} %bitcast.109), channel_id=1, replica_groups=mesh['sp'=4,'tp'=8] {'sp'}, dimensions={1} | all-to-all | bytes 1048576 | tf_op jit(solution)/shard_map/all_to_all | solution.py:42
  30.4 16.8 %all_to_all.49 = bf16[256,4,256]{2,0,1:T(8,128)(2,1)} all-to-all(bf16[256,4,256]{2,0,1:T(8,128)(2,1)S(1)} %bitcast.110), channel_id=1, replica_groups=mesh['sp'=4,'tp'=8] {'sp'}, dimensions={1} | all-to-all | bytes 1048576 | tf_op jit(solution)/shard_map/all_to_all | solution.py:43
  64.0 13.7 %all-to-all-done.1 = bf16[256,4,512]{0,2,1:T(8,128)(2,1)S(1)} async-done(((bf16[256,4,512]{0,2,1:T(8,128)(2,1)}), bf16[256,4,512]{0,2,1:T(8,128)(2,1)S(1)}, u32[]{:S(2)}, u32[]{:S(2)}) %all-to-all-start.1) | async-done | bytes 1048608 | tf_op jit(solution)/shard_map/all_to_all | solution.py:40
  124.2 18.2 %fusion.15 = f32[2,8192,256,2]{2,1,3,0:T(8,128)} fusion(bf16[256,2,2,128]{0,3,2,1:T(8,128)(2,1)} %bitcast.113, bf16[8192,2,128,1]{2,1,0,3:T(2,128)(2,1)} %bitcast.100), kind=kOutput, calls=%fused_computation.30 | convolution fusion | flops 2147483648 | bytes 38010880 | tf_op jit(solution)/shard_map/qhgd,khd->hgqk/dot_general | solution.py:16
  142.4 10.1 %fusion.23 = f32[2,6144,256,2]{2,1,3,0:T(8,128)} fusion(bf16[256,2,2,128]{0,3,2,1:T(8,128)(2,1)S(1)} %bitcast.112, bf16[6144,2,128,1]{2,1,0,3:T(2,128)(2,1)S(1)} %bitcast.101), kind=kOutput, calls=%fused_computation.39 | convolution fusion | flops 1610612736 | bytes 28573696 | tf_op jit(solution)/shard_map/qhgd,khd->hgqk/dot_general | solution.py:16
  152.4 8.1 fusion.30
  160.5 18.3 %fusion.71 = (f32[2,2,256]{2,1,0:T(2,128)S(1)}, f32[2,2,256,4096]{2,3,1,0:T(8,128)}) fusion(f32[2,4096,256,2]{2,1,3,0:T(8,128)} %fusion.30, pred[256,4096]{0,1:T(8,128)(4,1)S(1)} %copy-done.6), kind=kOutput, calls=%fused_computation.96 | output fusion | flops 25169920 | bytes 34607104 | tf_op jit(solution)/shard_map/sub | solution.py:22
  181.8 10.5 %broadcast_in_dim.53 = f32[2,2,256,6144]{2,3,1,0:T(8,128)} broadcast(f32[]{:T(128)} %constant.50.clone.1), dimensions={} | broadcast | bytes 25165828 | tf_op jit(solution)/shard_map/jit(_where)/broadcast_in_dim | solution.py:20
  192.3 10.5 %mul.80 = f32[2,6144,256,2]{2,1,3,0:T(8,128)} broadcast(f32[]{:T(128)} %constant.49.clone.1), dimensions={} | broadcast | bytes 25165828 | tf_op jit(solution)/shard_map/mul | solution.py:16
  202.8 56.1 %fusion.70 = (f32[2,2,256]{2,1,0:T(2,128)S(1)}, f32[2,2,256,6144]{2,3,1,0:T(8,128)}) fusion(pred[2,2,256,6144]{2,3,1,0:T(8,128)(4,1)S(1)} %broadcast_in_dim.52, f32[2,2,256,6144]{2,3,1,0:T(8,128)} %broadcast_in_dim.53, f32[2,6144,256,2]{2,1,3,0:T(8,128)} %fusion.23, f32[2,6144,256,2]{2,1,3,0:T(8,128)} %mul.80), kind=kOutput, calls=%fused_computation.95 | output fusion | flops 37754880 | bytes 106958848 | tf_op jit(solution)/shard_map/sub | solution.py:22
  258.9 11.8 %fusion.36 = bf16[2,2,256,128]{2,3,1,0:T(8,128)(2,1)} fusion(f32[2,2,256,6144]{2,3,1,0:T(8,128)} %get-tuple-element.15, f32[2,2,256]{2,1,0:T(2,128)S(1)} %get-tuple-element.14, bf16[6144,2,128,1]{2,1,0,3:T(2,128)(2,1)} %bitcast.105), kind=kOutput, calls=%fused_computation.56 | convolution fusion | flops 1623326720 | bytes 28577792 | tf_op jit(solution)/shard_map/hgqk,khd->qhgd/dot_general | solution.py:24
  270.7 8.2 fusion.33
  290.5 11.1 %broadcast_in_dim.77 = f32[2,2,256,8192]{2,3,1,0:T(8,128)} broadcast(f32[]{:T(128)} %constant.50.clone.1), dimensions={} | broadcast | bytes 33554436 | tf_op jit(solution)/shard_map/jit(_where)/broadcast_in_dim | solution.py:20
  301.7 11.0 %mul.83 = f32[2,8192,256,2]{2,1,3,0:T(8,128)} broadcast(f32[]{:T(128)} %constant.49.clone.1), dimensions={} | broadcast | bytes 33554436 | tf_op jit(solution)/shard_map/mul | solution.py:16
  312.6 78.0 %fusion.69 = (f32[2,2,256]{2,1,0:T(2,128)S(1)}, f32[2,2,256,8192]{2,3,1,0:T(8,128)}) fusion(pred[2,2,256,8192]{2,3,1,0:T(8,128)(4,1)} %broadcast_in_dim.76, f32[2,2,256,8192]{2,3,1,0:T(8,128)} %broadcast_in_dim.77, f32[2,8192,256,2]{2,1,3,0:T(8,128)} %fusion.15, f32[2,8192,256,2]{2,1,3,0:T(8,128)} %mul.83), kind=kOutput, calls=%fused_computation.94 | output fusion | flops 50339840 | bytes 142610432 | tf_op jit(solution)/shard_map/sub | solution.py:22
  401.7 13.5 %fusion.39 = bf16[2,2,256,128]{2,3,1,0:T(8,128)(2,1)S(1)} fusion(f32[2,2,256,8192]{2,3,1,0:T(8,128)} %get-tuple-element.13, f32[2,2,256]{2,1,0:T(2,128)S(1)} %get-tuple-element.12, bf16[8192,2,128,1]{2,1,0,3:T(2,128)(2,1)} %bitcast.103), kind=kOutput, calls=%fused_computation.57 | convolution fusion | flops 2164391936 | bytes 38014976 | tf_op jit(solution)/shard_map/hgqk,khd->qhgd/dot_general | solution.py:24
  422.0 76.5 %reduce-scatter.3.cloned.1.call-done = bf16[256,2048]{1,0:T(8,128)(2,1)} async-done(((bf16[1024,2048]{1,0:T(8,128)(2,1)}), bf16[256,2048]{1,0:T(8,128)(2,1)}) %reduce-scatter.3.cloned.1.call-update) | async-done | bytes 1048592 | tf_op jit(solution)/shard_map/reduce_scatter | solution.py:79
  503.1 69.4 %all-gather.16.cloned.1.call-done = bf16[2048,896]{1,0:T(8,128)(2,1)} async-done(((bf16[512,896]{1,0:T(8,128)(2,1)}), bf16[2048,896]{1,0:T(8,128)(2,1)}) %all-gather.16.cloned.1.call-update) | async-done | bytes 3670032 | tf_op jit(solution)/shard_map/all_gather | solution.py:96
  572.5 55.2 %all-gather.14.cloned.1.call-done = bf16[2048,2048]{1,0:T(8,128)(2,1)} async-done(((bf16[256,2048]{1,0:T(8,128)(2,1)}), bf16[2048,2048]{1,0:T(8,128)(2,1)}) %all-gather.14.cloned.1.call-update) | async-done | bytes 8388624 | tf_op jit(solution)/shard_map/all_gather | solution.py:91
  627.7 14.1 %fusion.73 = f32[2048,896]{1,0:T(8,128)} fusion(bf16[2048,2048]{1,0:T(8,128)(2,1)} %all-gather.14.cloned.1.call-done, bf16[2048,896]{1,0:T(8,128)(2,1)} %all-gather.16.cloned.1.call-done), kind=kOutput, calls=%fused_computation.98 | convolution fusion | flops 7516192768 | bytes 19398656 | tf_op jit(solution)/shard_map/dot_general | solution.py:29
  641.8 59.6 %all-gather.20.cloned.1.call-done = bf16[896,2048]{1,0:T(8,128)(2,1)} async-done(((bf16[896,512]{1,0:T(8,128)(2,1)}), bf16[896,2048]{1,0:T(8,128)(2,1)}) %all-gather.20.cloned.1.call-update) | async-done | bytes 3670032 | tf_op jit(solution)/shard_map/all_gather | solution.py:99
  701.4 72.3 %all-gather.18.cloned.1.call-done = bf16[2048,896]{1,0:T(8,128)(2,1)} async-done(((bf16[512,896]{1,0:T(8,128)(2,1)}), bf16[2048,896]{1,0:T(8,128)(2,1)}) %all-gather.18.cloned.1.call-update) | async-done | bytes 3670032 | tf_op jit(solution)/shard_map/all_gather | solution.py:97
  773.6 25.3 %convolution_convert_fusion = bf16[2048,2048]{1,0:T(8,128)(2,1)} fusion(bf16[896,2048]{1,0:T(8,128)(2,1)} %all-gather.20.cloned.1.call-done, f32[2048,896]{1,0:T(8,128)} %fusion.73, bf16[2048,2048]{1,0:T(8,128)(2,1)} %all-gather.14.cloned.1.call-done, bf16[2048,896]{1,0:T(8,128)(2,1)} %all-gather.18.cloned.1.call-done), kind=kOutput, calls=%fused_computation.26 | convolution fusion | flops 15047589888 | bytes 31457280 | tf_op jit(solution)/shard_map/dot_general | solution.py:102
  799.0 70.2 %reduce-scatter.5.cloned.1.call-done = bf16[256,2048]{1,0:T(8,128)(2,1)} async-done(((bf16[2048,2048]{1,0:T(8,128)(2,1)}), bf16[256,2048]{1,0:T(8,128)(2,1)}) %reduce-scatter.5.cloned.1.call-update) | async-done | bytes 1048592 | tf_op jit(solution)/shard_map/reduce_scatter | solution.py:101
  (92 shorter events, 105.2 us)
Async XLA Ops:
  7.2 71.5 %all-gather.8.cloned.1.call-start = ((), (), s32[]{:S(2)}) async-start(), calls=%async_computation.5 | async-start | bytes 4718592 | tf_op jit(solution)/shard_map/all_gather | solution.py:47
  29.2 75.1 %all-gather.10.cloned.1.call-start = ((), (), s32[]{:S(2)}) async-start(), calls=%async_computation.6 | async-start | bytes 4718592 | tf_op jit(solution)/shard_map/all_gather | solution.py:48
  49.4 28.3 %all-to-all-start.1 = ((bf16[256,4,512]{0,2,1:T(8,128)(2,1)}), bf16[256,4,512]{0,2,1:T(8,128)(2,1)S(1)}, u32[]{:S(2)}, u32[]{:S(2)}) async-start(bf16[256,4,512]{0,2,1:T(8,128)(2,1)} %bitcast.4), calls=%async_computation.1 | async-start | bytes 2097152 | tf_op jit(solution)/shard_map/all_to_all | solution.py:40
  53.0 362.3 %all-gather.12.cloned.1.call-start = ((), (), s32[]{:S(2)}) async-start(), calls=%async_computation.7 | async-start | bytes 2359296 | tf_op jit(solution)/shard_map/all_gather | solution.py:77
  53.7 444.7 %reduce-scatter.3.cloned.1.call-start = ((), (), s32[]{:S(2)}) async-start(), calls=%async_computation.8 | async-start | bytes 5242880 | tf_op jit(solution)/shard_map/reduce_scatter | solution.py:79
  84.8 7.2 slice-start.3
  112.5 8.2 slice-start.1
  124.2 18.2 %copy-start = (bf16[6144,2,128]{2,1,0:T(2,128)(2,1)S(1)}, bf16[6144,2,128]{2,1,0:T(2,128)(2,1)}, u32[]{:S(2)}) copy-start(bf16[6144,2,128]{2,1,0:T(2,128)(2,1)} %reshape.205) | copy-start | bytes 9437188
  124.2 18.2 %copy-start.5 = (bf16[1,256,512]{1,2,0:T(8,128)(2,1)S(1)}, bf16[1,256,512]{1,2,0:T(8,128)(2,1)}, u32[]{:S(2)}) copy-start(bf16[1,256,512]{1,2,0:T(8,128)(2,1)} %get-tuple-element.6) | copy-start | bytes 786436
  142.4 10.1 %copy-start.3 = (bf16[4096,2,128]{2,1,0:T(2,128)(2,1)S(1)}, bf16[4096,2,128]{2,1,0:T(2,128)(2,1)}, u32[]{:S(2)}) copy-start(bf16[4096,2,128]{2,1,0:T(2,128)(2,1)} %reshape.201) | copy-start | bytes 6291460
  152.4 8.1 copy-start.6
  258.9 11.8 %copy-start.4 = (bf16[4096,2,128]{2,1,0:T(2,128)(2,1)S(1)}, bf16[4096,2,128]{2,1,0:T(2,128)(2,1)}, u32[]{:S(2)}) copy-start(bf16[4096,2,128]{2,1,0:T(2,128)(2,1)} %reshape.219) | copy-start | bytes 6291460
  270.7 8.2 slice-start.4
  270.7 8.2 copy-start.9
  312.6 78.0 %copy-start.8 = (bf16[1,2048,256]{1,2,0:T(8,128)(2,1)S(1)}, bf16[1,2048,256]{1,2,0:T(8,128)(2,1)}, u32[]{:S(2)}) copy-start(bf16[1,2048,256]{1,2,0:T(8,128)(2,1)} %copy.24) | copy-start | bytes 3145732
  401.7 13.6 %copy-start.11 = (bf16[2,2,256,128]{2,3,1,0:T(8,128)(2,1)S(1)}, bf16[2,2,256,128]{2,3,1,0:T(8,128)(2,1)}, u32[]{:S(2)}) copy-start(bf16[2,2,256,128]{2,3,1,0:T(8,128)(2,1)} %fusion.36) | copy-start | bytes 786436
  401.7 13.6 %copy-start.12 = (bf16[2,2,256,128]{2,3,1,0:T(8,128)(2,1)S(1)}, bf16[2,2,256,128]{2,3,1,0:T(8,128)(2,1)}, u32[]{:S(2)}) copy-start(bf16[2,2,256,128]{2,3,1,0:T(8,128)(2,1)} %fusion.33) | copy-start | bytes 786436
  415.3 83.2 %copy-start.7 = (bf16[256,2048]{1,0:T(8,128)(2,1)S(1)}, bf16[256,2048]{1,0:T(8,128)(2,1)}, u32[]{:S(2)}) copy-start(bf16[256,2048]{1,0:T(8,128)(2,1)} %param.9) | copy-start | bytes 3145732
  421.3 151.2 %all-gather.16.cloned.1.call-start = ((), (), s32[]{:S(2)}) async-start(), calls=%async_computation.10 | async-start | bytes 4587520 | tf_op jit(solution)/shard_map/all_gather | solution.py:96
  421.9 205.8 %all-gather.14.cloned.1.call-start = ((), (), s32[]{:S(2)}) async-start(), calls=%async_computation.9 | async-start | bytes 9437184 | tf_op jit(solution)/shard_map/all_gather | solution.py:91
  500.2 369.0 %copy-start.1 = (bf16[256,2048]{1,0:T(8,128)(2,1)}, bf16[256,2048]{1,0:T(8,128)(2,1)S(1)}, u32[]{:S(2)}) copy-start(bf16[256,2048]{1,0:T(8,128)(2,1)S(1)} %get-tuple-element.3) | copy-start | bytes 3145732
  501.5 199.8 %all-gather.20.cloned.1.call-start = ((), (), s32[]{:S(2)}) async-start(), calls=%async_computation.12 | async-start | bytes 4587520 | tf_op jit(solution)/shard_map/all_gather | solution.py:99
  502.3 271.4 %all-gather.18.cloned.1.call-start = ((), (), s32[]{:S(2)}) async-start(), calls=%async_computation.11 | async-start | bytes 4587520 | tf_op jit(solution)/shard_map/all_gather | solution.py:97
  503.0 366.2 %reduce-scatter.5.cloned.1.call-start = ((), (), s32[]{:S(2)}) async-start(), calls=%async_computation.13 | async-start | bytes 9437184 | tf_op jit(solution)/shard_map/reduce_scatter | solution.py:101
  (4 other events, 21.0 us)
Sparse Core Ops, SparseCore 0:
  29.3 36.4 all-gather.7
  67.7 36.5 all-gather.9
  106.2 28.0 all-gather.11
  421.4 76.9 reduce-scatter.2
  499.9 72.5 all-gather.15
  574.8 52.8 all-gather.13
  629.3 72.0 all-gather.19
  702.9 70.6 all-gather.17
  799.1 70.0 reduce-scatter.4
where the time goes:
time: 882 us; the launch traced here: 879 us
  waiting for transfers between devices  424 us (48%)
  other arithmetic  168 us (19%)
  matrix products  126 us (14%)
  local copies, waits for them, and re-layouts  105 us (12%)
  blocking collectives  37.5 us (4%)
  between operations  14.2 us (2%)
    sub x3, other arithmetic, attend(): exp_terms = jnp.exp(scores - row_peak)  152 us
    reduce_scatter x1, waiting for transfers between devices, shards(): lax.psum_scatter(jnp.dot(block_rows, wo_full, preferred_element_type=jnp....  76.5 us
    all_gather x1, waiting for transfers between devices, shards(): up_sum = add_single(lax.all_gather(up_weight, 'sp', axis=0, tiled=True))  72.3 us
    reduce_scatter x1, waiting for transfers between devices, shards(): lax.psum_scatter(jnp.dot(block_rows, down_full, preferred_element_type=jn...  70.2 us
    all_gather x1, waiting for transfers between devices, shards(): gate_sum = add_single(lax.all_gather(gate_weight, 'sp', axis=0, tiled=True))  69.4 us
    all_gather x1, waiting for transfers between devices, shards(): down_full = lax.all_gather(down_weight, 'sp', axis=1, tiled=True)  59.6 us
    all_gather x1, waiting for transfers between devices, shards(): all_rows = lax.all_gather(normed, 'tp', axis=0, tiled=True)  55.2 us
    dot_general x4, matrix products, attend(): jnp.einsum('hgqk,khd->qhgd', probs, v_three, preferred_element_type=jnp.f...  37.6 us
  transfers between devices with their start and end apart: 10, of which 8 were waited for; matrix products, arithmetic and copies ran while one was open for 41% of the time, Pallas kernels for 0%

commit v1 on v0

--- a/solution.py
+++ b/solution.py
@@ -5,6 +5,17 @@
 
 HEAD_DIM = 128
 norm_eps = 1e-05
+
+
+def gather_by_hops(array, axis, dim):
+    size = lax.axis_size(axis)
+    right = [(i, (i + 1) % size) for i in range(size)]
+    parts = [array]
+    for stride in range(1, size):
+        parts = [lax.ppermute(parts[0], axis, right), *parts]
+    whole = jnp.concatenate(parts, axis=dim)
+    offset = (lax.axis_index(axis) + 1) * parts[-1].shape[dim]
+    return jnp.roll(whole, offset, axis=dim)
 
 
 def attend(q_block, query_pos, k_block, v_block, key_pos, kv_local):
@@ -88,7 +99,7 @@
         jnp.mean(attended_wide * attended_wide, axis=1, keepdims=True) + norm_eps
     )
     normed = (attended_wide * inverse_rms * norm_gain.astype(jnp.float32)).astype(jnp.bfloat16)
-    all_rows = lax.all_gather(normed, "tp", axis=0, tiled=True)
+    all_rows = gather_by_hops(normed, "tp", 0)
 
     def add_single(weight_piece):
         return add_rows(all_rows, weight_piece)

time: 882 us -> 826 us (0.937)
  waiting for transfers between devices: 424 us -> 339 us
  local copies, waits for them, and re-layouts: 105 us -> 131 us
    ppermute x0 -> x7, waiting for transfers between devices: none -> 106 us  [gather_by_hops(): parts = [lax.ppermute(parts[0], axis, right), *parts]]
    all_gather x1, waiting for transfers between devices: 72.3 us -> 0.01 us  [shards(): up_sum = add_single(lax.all_gather(up_weight, 'sp', axis=0, tiled=True))]
    all_gather x1, waiting for transfers between devices: 59.6 us -> 0.01 us  [shards(): down_full = lax.all_gather(down_weight, 'sp', axis=1, tiled=True)]
    all_gather x1 -> x0, waiting for transfers between devices: 55.2 us -> none  [shards(): all_rows = lax.all_gather(normed, 'tp', axis=0, tiled=True)]
    unnamed x28 -> x54, local copies, waits for them, and re-layouts: 3.56 us -> 29.3 us
  transfers between devices with their start and end apart: 10 -> 16, of which waited for: 8 -> 12; matrix products, arithmetic and copies ran while one was open for 41% -> 47% of each run, Pallas kernels for 0% -> 0%
where the time goes in v1:
time: 826 us; the launch traced here: 822 us
  waiting for transfers between devices  339 us (41%)
  other arithmetic  170 us (21%)
  local copies, waits for them, and re-layouts  131 us (16%)
  matrix products  126 us (15%)
  blocking collectives  37.5 us (5%)
  between operations  14.6 us (2%)
    sub x3, other arithmetic, attend(): exp_terms = jnp.exp(scores - row_peak)  152 us
    ppermute x7, waiting for transfers between devices, gather_by_hops(): parts = [lax.ppermute(parts[0], axis, right), *parts]  106 us
    reduce_scatter x1, waiting for transfers between devices, shards(): lax.psum_scatter(jnp.dot(block_rows, wo_full, preferred_element_type=jnp....  76.5 us
    reduce_scatter x1, waiting for transfers between devices, shards(): lax.psum_scatter(jnp.dot(block_rows, down_full, preferred_element_type=jn...  70.2 us
    all_gather x1, waiting for transfers between devices, shards(): gate_sum = add_single(lax.all_gather(gate_weight, 'sp', axis=0, tiled=True))  67.3 us
    dot_general x4, matrix products, attend(): jnp.einsum('hgqk,khd->qhgd', probs, v_three, preferred_element_type=jnp.f...  37.6 us
    dot_general x3, matrix products, attend(): jnp.einsum('qhgd,khd->hgqk', q_four, k_three, preferred_element_type=jnp....  36.4 us
    broadcast_in_dim x4, local copies, waits for them, and re-layouts, attend(): scores = jnp.where(causal[None, None, :, :], scores, -1e+30)  30 us
  transfers between devices with their start and end apart: 16, of which 12 were waited for; matrix products, arithmetic and copies ran while one was open for 47% of the time, Pallas kernels for 0%

profile of v1, /device:TPU:0, one launch (start us, length us, event | category | flops | bytes accessed | tf_op | source)
XLA Modules:
  0.0 822.1 jit_solution(10945971961109001587)
XLA Ops:
  8.5 20.7 %all_to_all.48 = bf16[256,4,256]{0,2,1:T(8,128)(2,1)} all-to-all(bf16[256,4,256]{0,2,1:T(8,128)(2,1)S(1)} %bitcast.107), channel_id=1, replica_groups=mesh['sp'=4,'tp'=8] {'sp'}, dimensions={1} | all-to-all | bytes 1048576 | tf_op jit(solution)/shard_map/all_to_all | solution.py:53
  30.4 16.8 %all_to_all.49 = bf16[256,4,256]{2,0,1:T(8,128)(2,1)} all-to-all(bf16[256,4,256]{2,0,1:T(8,128)(2,1)S(1)} %bitcast.108), channel_id=1, replica_groups=mesh['sp'=4,'tp'=8] {'sp'}, dimensions={1} | all-to-all | bytes 1048576 | tf_op jit(solution)/shard_map/all_to_all | solution.py:54
  64.1 13.6 %all-to-all-done.1 = bf16[256,4,512]{0,2,1:T(8,128)(2,1)S(1)} async-done(((bf16[256,4,512]{0,2,1:T(8,128)(2,1)}), bf16[256,4,512]{0,2,1:T(8,128)(2,1)S(1)}, u32[]{:S(2)}, u32[]{:S(2)}) %all-to-all-start.1) | async-done | bytes 1048608 | tf_op jit(solution)/shard_map/all_to_all | solution.py:51
  124.1 18.2 %fusion.19 = f32[2,8192,256,2]{2,1,3,0:T(8,128)} fusion(bf16[256,2,2,128]{0,3,2,1:T(8,128)(2,1)} %bitcast.111, bf16[8192,2,128,1]{2,1,0,3:T(2,128)(2,1)} %bitcast.98), kind=kOutput, calls=%fused_computation.34 | convolution fusion | flops 2147483648 | bytes 38010880 | tf_op jit(solution)/shard_map/qhgd,khd->hgqk/dot_general | solution.py:27
  160.5 18.2 %fusion.82 = (f32[2,2,256]{2,1,0:T(2,128)S(1)}, f32[2,2,256,4096]{2,3,1,0:T(8,128)}) fusion(f32[2,4096,256,2]{2,1,3,0:T(8,128)} %fusion.38, pred[256,4096]{0,1:T(8,128)(4,1)S(1)} %copy-done.12), kind=kOutput, calls=%fused_computation.118 | output fusion | flops 25169920 | bytes 34607104 | tf_op jit(solution)/shard_map/sub | solution.py:33
  181.8 10.5 %broadcast_in_dim.53 = f32[2,2,256,6144]{2,3,1,0:T(8,128)} broadcast(f32[]{:T(128)} %constant.69.clone.1), dimensions={} | broadcast | bytes 25165828 | tf_op jit(solution)/shard_map/jit(_where)/broadcast_in_dim | solution.py:31
  202.7 56.0 %fusion.81 = (f32[2,2,256]{2,1,0:T(2,128)S(1)}, f32[2,2,256,6144]{2,3,1,0:T(8,128)}) fusion(pred[2,2,256,6144]{2,3,1,0:T(8,128)(4,1)S(1)} %broadcast_in_dim.52, f32[2,2,256,6144]{2,3,1,0:T(8,128)} %broadcast_in_dim.53, f32[2,6144,256,2]{2,1,3,0:T(8,128)} %fusion.31, f32[2,6144,256,2]{2,1,3,0:T(8,128)} %mul.83), kind=kOutput, calls=%fused_computation.117 | output fusion | flops 37754880 | bytes 106958848 | tf_op jit(solution)/shard_map/sub | solution.py:33
  258.8 11.8 %fusion.44 = bf16[2,2,256,128]{2,3,1,0:T(8,128)(2,1)} fusion(f32[2,2,256,6144]{2,3,1,0:T(8,128)} %get-tuple-element.15, f32[2,2,256]{2,1,0:T(2,128)S(1)} %get-tuple-element.14, bf16[6144,2,128,1]{2,1,0,3:T(2,128)(2,1)} %bitcast.103), kind=kOutput, calls=%fused_computation.60 | convolution fusion | flops 1623326720 | bytes 28577792 | tf_op jit(solution)/shard_map/hgqk,khd->qhgd/dot_general | solution.py:35
  290.4 11.1 %broadcast_in_dim.77 = f32[2,2,256,8192]{2,3,1,0:T(8,128)} broadcast(f32[]{:T(128)} %constant.69.clone.1), dimensions={} | broadcast | bytes 33554436 | tf_op jit(solution)/shard_map/jit(_where)/broadcast_in_dim | solution.py:31
  301.5 11.0 %mul.86 = f32[2,8192,256,2]{2,1,3,0:T(8,128)} broadcast(f32[]{:T(128)} %constant.68.clone.1), dimensions={} | broadcast | bytes 33554436 | tf_op jit(solution)/shard_map/mul | solution.py:27
  312.5 78.0 %fusion.80 = (f32[2,2,256]{2,1,0:T(2,128)S(1)}, f32[2,2,256,8192]{2,3,1,0:T(8,128)}) fusion(pred[2,2,256,8192]{2,3,1,0:T(8,128)(4,1)} %broadcast_in_dim.76, f32[2,2,256,8192]{2,3,1,0:T(8,128)} %broadcast_in_dim.77, f32[2,8192,256,2]{2,1,3,0:T(8,128)} %fusion.19, f32[2,8192,256,2]{2,1,3,0:T(8,128)} %mul.86), kind=kOutput, calls=%fused_computation.116 | output fusion | flops 50339840 | bytes 142610432 | tf_op jit(solution)/shard_map/sub | solution.py:33
  401.5 13.5 %fusion.47 = bf16[2,2,256,128]{2,3,1,0:T(8,128)(2,1)S(1)} fusion(f32[2,2,256,8192]{2,3,1,0:T(8,128)} %get-tuple-element.13, f32[2,2,256]{2,1,0:T(2,128)S(1)} %get-tuple-element.12, bf16[8192,2,128,1]{2,1,0,3:T(2,128)(2,1)} %bitcast.101), kind=kOutput, calls=%fused_computation.61 | convolution fusion | flops 2164391936 | bytes 38014976 | tf_op jit(solution)/shard_map/hgqk,khd->qhgd/dot_general | solution.py:35
  421.8 76.5 %reduce-scatter.3.cloned.1.call-done = bf16[256,2048]{1,0:T(8,128)(2,1)} async-done(((bf16[1024,2048]{1,0:T(8,128)(2,1)}), bf16[256,2048]{1,0:T(8,128)(2,1)}) %reduce-scatter.3.cloned.1.call-update) | async-done | bytes 1048592 | tf_op jit(solution)/shard_map/reduce_scatter | solution.py:90
  500.5 15.1 %collective-permute-done = bf16[256,2048]{1,0:T(8,128)(2,1)S(1)} collective-permute-done((bf16[256,2048]{1,0:T(8,128)(2,1)S(1)}, bf16[256,2048]{1,0:T(8,128)(2,1)S(1)}, u32[]{:S(2)}, u32[]{:S(2)}) %collective-permute-start) | collective-permute-done | bytes 1048608 | tf_op jit(solution)/shard_map/ppermute | solution.py:15
  515.7 15.0 %collective-permute-done.1 = bf16[256,2048]{1,0:T(8,128)(2,1)S(1)} collective-permute-done((bf16[256,2048]{1,0:T(8,128)(2,1)S(1)}, bf16[256,2048]{1,0:T(8,128)(2,1)S(1)}, u32[]{:S(2)}, u32[]{:S(2)}) %collective-permute-start.1) | collective-permute-done | bytes 1048608 | tf_op jit(solution)/shard_map/ppermute | solution.py:15
  530.7 15.1 %collective-permute-done.2 = bf16[256,2048]{1,0:T(8,128)(2,1)S(1)} collective-permute-done((bf16[256,2048]{1,0:T(8,128)(2,1)S(1)}, bf16[256,2048]{1,0:T(8,128)(2,1)S(1)}, u32[]{:S(2)}, u32[]{:S(2)}) %collective-permute-start.2) | collective-permute-done | bytes 1048608 | tf_op jit(solution)/shard_map/ppermute | solution.py:15
  546.8 15.1 %collective-permute-done.3 = bf16[256,2048]{1,0:T(8,128)(2,1)S(1)} collective-permute-done((bf16[256,2048]{1,0:T(8,128)(2,1)S(1)}, bf16[256,2048]{1,0:T(8,128)(2,1)S(1)}, u32[]{:S(2)}, u32[]{:S(2)}) %collective-permute-start.3) | collective-permute-done | bytes 1048608 | tf_op jit(solution)/shard_map/ppermute | solution.py:15
  562.9 15.1 %collective-permute-done.4 = bf16[256,2048]{1,0:T(8,128)(2,1)S(1)} collective-permute-done((bf16[256,2048]{1,0:T(8,128)(2,1)S(1)}, bf16[256,2048]{1,0:T(8,128)(2,1)S(1)}, u32[]{:S(2)}, u32[]{:S(2)}) %collective-permute-start.4) | collective-permute-done | bytes 1048608 | tf_op jit(solution)/shard_map/ppermute | solution.py:15
  579.0 15.2 %collective-permute-done.5 = bf16[256,2048]{1,0:T(8,128)(2,1)} collective-permute-done((bf16[256,2048]{1,0:T(8,128)(2,1)S(1)}, bf16[256,2048]{1,0:T(8,128)(2,1)}, u32[]{:S(2)}, u32[]{:S(2)}) %collective-permute-start.5) | collective-permute-done | bytes 1048608 | tf_op jit(solution)/shard_map/ppermute | solution.py:15
  594.4 15.3 %collective-permute-done.6 = bf16[256,2048]{1,0:T(8,128)(2,1)} collective-permute-done((bf16[256,2048]{1,0:T(8,128)(2,1)}, bf16[256,2048]{1,0:T(8,128)(2,1)}, u32[]{:S(2)}, u32[]{:S(2)}) %collective-permute-start.6) | collective-permute-done | bytes 1048608 | tf_op jit(solution)/shard_map/ppermute | solution.py:15
  635.2 14.3 %fusion.13 = f32[2048,896]{1,0:T(8,128)} fusion(bf16[2048,896]{1,0:T(8,128)(2,1)} %all-gather.15.cloned.1.call-done, bf16[4096,2048]{1,0:T(8,128)(2,1)} %constant_dynamic-update-slice_fusion, s32[]{:T(128)S(6)} %select_n.47), kind=kOutput, calls=%fused_computation.27 | convolution fusion | flops 7516192768 | bytes 19398660 | tf_op jit(solution)/shard_map/dot_general | solution.py:40
  649.5 67.3 %all-gather.13.cloned.1.call-done = bf16[2048,896]{1,0:T(8,128)(2,1)} async-done(((bf16[512,896]{1,0:T(8,128)(2,1)}), bf16[2048,896]{1,0:T(8,128)(2,1)}) %all-gather.13.cloned.1.call-update) | async-done | bytes 3670032 | tf_op jit(solution)/shard_map/all_gather | solution.py:107
  716.8 25.5 %convolution_convert_fusion = bf16[2048,2048]{1,0:T(8,128)(2,1)} fusion(bf16[896,2048]{1,0:T(8,128)(2,1)} %all-gather.17.cloned.1.call-done, f32[2048,896]{1,0:T(8,128)} %fusion.13, bf16[2048,896]{1,0:T(8,128)(2,1)} %all-gather.13.cloned.1.call-done, bf16[4096,2048]{1,0:T(8,128)(2,1)} %constant_dynamic-update-slice_fusion, s32[]{:T(128)S(6)} %select_n.47), kind=kOutput, calls=%fused_computation.26 | convolution fusion | flops 15047589888 | bytes 31457284 | tf_op jit(solution)/shard_map/dot_general | solution.py:113
  742.3 70.2 %reduce-scatter.5.cloned.1.call-done = bf16[256,2048]{1,0:T(8,128)(2,1)} async-done(((bf16[2048,2048]{1,0:T(8,128)(2,1)}), bf16[256,2048]{1,0:T(8,128)(2,1)}) %reduce-scatter.5.cloned.1.call-update) | async-done | bytes 1048592 | tf_op jit(solution)/shard_map/reduce_scatter | solution.py:112
  (131 shorter events, 168.2 us)
Async XLA Ops:
  7.2 71.5 %all-gather.7.cloned.1.call-start = ((), (), s32[]{:S(2)}) async-start(), calls=%async_computation.5 | async-start | bytes 4718592 | tf_op jit(solution)/shard_map/all_gather | solution.py:58
  29.2 75.1 %all-gather.9.cloned.1.call-start = ((), (), s32[]{:S(2)}) async-start(), calls=%async_computation.6 | async-start | bytes 4718592 | tf_op jit(solution)/shard_map/all_gather | solution.py:59
  49.4 28.3 %all-to-all-start.1 = ((bf16[256,4,512]{0,2,1:T(8,128)(2,1)}), bf16[256,4,512]{0,2,1:T(8,128)(2,1)S(1)}, u32[]{:S(2)}, u32[]{:S(2)}) async-start(bf16[256,4,512]{0,2,1:T(8,128)(2,1)} %bitcast.4), calls=%async_computation.1 | async-start | bytes 2097152 | tf_op jit(solution)/shard_map/all_to_all | solution.py:51
  53.0 362.1 %all-gather.11.cloned.1.call-start = ((), (), s32[]{:S(2)}) async-start(), calls=%async_computation.7 | async-start | bytes 2359296 | tf_op jit(solution)/shard_map/all_gather | solution.py:88
  53.7 444.6 %reduce-scatter.3.cloned.1.call-start = ((), (), s32[]{:S(2)}) async-start(), calls=%async_computation.8 | async-start | bytes 5242880 | tf_op jit(solution)/shard_map/reduce_scatter | solution.py:90
  124.1 18.2 %copy-start.1 = (bf16[6144,2,128]{2,1,0:T(2,128)(2,1)S(1)}, bf16[6144,2,128]{2,1,0:T(2,128)(2,1)}, u32[]{:S(2)}) copy-start(bf16[6144,2,128]{2,1,0:T(2,128)(2,1)} %reshape.205) | copy-start | bytes 9437188
  124.1 18.2 %copy-start.11 = (bf16[1,256,512]{1,2,0:T(8,128)(2,1)S(1)}, bf16[1,256,512]{1,2,0:T(8,128)(2,1)}, u32[]{:S(2)}) copy-start(bf16[1,256,512]{1,2,0:T(8,128)(2,1)} %get-tuple-element.6) | copy-start | bytes 786436
  312.5 78.0 %copy-start.14 = (bf16[1,2048,256]{1,2,0:T(8,128)(2,1)S(1)}, bf16[1,2048,256]{1,2,0:T(8,128)(2,1)}, u32[]{:S(2)}) copy-start(bf16[1,2048,256]{1,2,0:T(8,128)(2,1)} %copy.24) | copy-start | bytes 3145732
  401.5 13.6 %copy-start.18 = (bf16[2,2,256,128]{2,3,1,0:T(8,128)(2,1)S(1)}, bf16[2,2,256,128]{2,3,1,0:T(8,128)(2,1)}, u32[]{:S(2)}) copy-start(bf16[2,2,256,128]{2,3,1,0:T(8,128)(2,1)} %fusion.41) | copy-start | bytes 786436
  415.1 83.2 %copy-start.13 = (bf16[256,2048]{1,0:T(8,128)(2,1)S(1)}, bf16[256,2048]{1,0:T(8,128)(2,1)}, u32[]{:S(2)}) copy-start(bf16[256,2048]{1,0:T(8,128)(2,1)} %param.9) | copy-start | bytes 3145732
  421.2 214.0 %all-gather.15.cloned.1.call-start = ((), (), s32[]{:S(2)}) async-start(), calls=%async_computation.10 | async-start | bytes 4587520 | tf_op jit(solution)/shard_map/all_gather | solution.py:108
  421.8 227.7 %all-gather.17.cloned.1.call-start = ((), (), s32[]{:S(2)}) async-start(), calls=%async_computation.11 | async-start | bytes 4587520 | tf_op jit(solution)/shard_map/all_gather | solution.py:110
  500.1 312.4 %copy-start = (bf16[256,2048]{1,0:T(8,128)(2,1)}, bf16[256,2048]{1,0:T(8,128)(2,1)S(1)}, u32[]{:S(2)}) copy-start(bf16[256,2048]{1,0:T(8,128)(2,1)S(1)} %get-tuple-element.3) | copy-start | bytes 3145732
  500.4 15.2 %collective-permute-start = (bf16[256,2048]{1,0:T(8,128)(2,1)S(1)}, bf16[256,2048]{1,0:T(8,128)(2,1)S(1)}, u32[]{:S(2)}, u32[]{:S(2)}) collective-permute-start(bf16[256,2048]{1,0:T(8,128)(2,1)S(1)} %fusion.35), channel_id=1, source_target_pairs={{0,1},{1,2},{2,3},{3,4},{4,5},{5,6},{6,7},{7,0},{8,9},{9,10},{10,1... | collective-permute-start | bytes 3145736 | tf_op jit(solution)/shard_map/ppermute | solution.py:15
  515.6 15.1 %collective-permute-start.1 = (bf16[256,2048]{1,0:T(8,128)(2,1)S(1)}, bf16[256,2048]{1,0:T(8,128)(2,1)S(1)}, u32[]{:S(2)}, u32[]{:S(2)}) collective-permute-start(bf16[256,2048]{1,0:T(8,128)(2,1)S(1)} %collective-permute-done), channel_id=1, source_target_pairs={{0,1},{1,2},{2,3},{3,4},{4,5},{5,6},{6,7},{7,0},{8,9},{9,10},{10,1... | collective-permute-start | bytes 3145736 | tf_op jit(solution)/shard_map/ppermute | solution.py:15
  515.6 201.2 %all-gather.13.cloned.1.call-start = ((), (), s32[]{:S(2)}) async-start(), calls=%async_computation.9 | async-start | bytes 4587520 | tf_op jit(solution)/shard_map/all_gather | solution.py:107
  530.7 15.1 %collective-permute-start.2 = (bf16[256,2048]{1,0:T(8,128)(2,1)S(1)}, bf16[256,2048]{1,0:T(8,128)(2,1)S(1)}, u32[]{:S(2)}, u32[]{:S(2)}) collective-permute-start(bf16[256,2048]{1,0:T(8,128)(2,1)S(1)} %collective-permute-done.1), channel_id=1, source_target_pairs={{0,1},{1,2},{2,3},{3,4},{4,5},{5,6},{6,7},{7,0},{8,9},{9,10},{10,1... | collective-permute-start | bytes 3145736 | tf_op jit(solution)/shard_map/ppermute | solution.py:15
  546.8 15.1 %collective-permute-start.3 = (bf16[256,2048]{1,0:T(8,128)(2,1)S(1)}, bf16[256,2048]{1,0:T(8,128)(2,1)S(1)}, u32[]{:S(2)}, u32[]{:S(2)}) collective-permute-start(bf16[256,2048]{1,0:T(8,128)(2,1)S(1)} %collective-permute-done.2), channel_id=1, source_target_pairs={{0,1},{1,2},{2,3},{3,4},{4,5},{5,6},{6,7},{7,0},{8,9},{9,10},{10,1... | collective-permute-start | bytes 3145736 | tf_op jit(solution)/shard_map/ppermute | solution.py:15
  562.9 15.1 %collective-permute-start.4 = (bf16[256,2048]{1,0:T(8,128)(2,1)S(1)}, bf16[256,2048]{1,0:T(8,128)(2,1)S(1)}, u32[]{:S(2)}, u32[]{:S(2)}) collective-permute-start(bf16[256,2048]{1,0:T(8,128)(2,1)S(1)} %collective-permute-done.3), channel_id=1, source_target_pairs={{0,1},{1,2},{2,3},{3,4},{4,5},{5,6},{6,7},{7,0},{8,9},{9,10},{10,1... | collective-permute-start | bytes 3145736 | tf_op jit(solution)/shard_map/ppermute | solution.py:15
  579.0 15.2 %collective-permute-start.5 = (bf16[256,2048]{1,0:T(8,128)(2,1)S(1)}, bf16[256,2048]{1,0:T(8,128)(2,1)}, u32[]{:S(2)}, u32[]{:S(2)}) collective-permute-start(bf16[256,2048]{1,0:T(8,128)(2,1)S(1)} %collective-permute-done.4), channel_id=1, source_target_pairs={{0,1},{1,2},{2,3},{3,4},{4,5},{5,6},{6,7},{7,0},{8,9},{9,10},{10,1... | collective-permute-start | bytes 3145736 | tf_op jit(solution)/shard_map/ppermute | solution.py:15
  594.3 15.4 %collective-permute-start.6 = (bf16[256,2048]{1,0:T(8,128)(2,1)}, bf16[256,2048]{1,0:T(8,128)(2,1)}, u32[]{:S(2)}, u32[]{:S(2)}) collective-permute-start(bf16[256,2048]{1,0:T(8,128)(2,1)} %collective-permute-done.5), channel_id=1, source_target_pairs={{0,1},{1,2},{2,3},{3,4},{4,5},{5,6},{6,7},{7,0},{8,9},{9,10},{10,1... | collective-permute-start | bytes 3145736 | tf_op jit(solution)/shard_map/ppermute | solution.py:15
  594.3 218.2 %reduce-scatter.5.cloned.1.call-start = ((), (), s32[]{:S(2)}) async-start(), calls=%async_computation.12 | async-start | bytes 9437184 | tf_op jit(solution)/shard_map/reduce_scatter | solution.py:112
  594.4 24.8 %copy-start.5 = (bf16[256,2048]{1,0:T(8,128)(2,1)S(1)}, bf16[256,2048]{1,0:T(8,128)(2,1)}, u32[]{:S(2)}) copy-start(bf16[256,2048]{1,0:T(8,128)(2,1)} %copy-done.4) | copy-start | bytes 3145732
  614.3 14.1 %copy-start.9 = (bf16[256,2048]{1,0:T(8,128)(2,1)S(1)}, bf16[256,2048]{1,0:T(8,128)(2,1)}, u32[]{:S(2)}) copy-start(bf16[256,2048]{1,0:T(8,128)(2,1)} %copy-done.8) | copy-start | bytes 3145732
  (16 other events, 115.2 us)
Sparse Core Ops, SparseCore 0:
  29.3 36.4 all-gather.6
  67.7 36.5 all-gather.8
  106.2 28.0 all-gather.10
  421.3 77.0 reduce-scatter.2
  499.8 72.5 all-gather.14
  573.8 70.6 all-gather.16
  646.1 70.6 all-gather.12
  742.4 70.0 reduce-scatter.4
